TPU v7x, 256 devices: a whole 4x4x8 slice. The times are simulated.
256 devices in a mesh: dp: 8 (over x, core), expert: 32 (over y, z).
Axes of the slice: x: 4, y: 4, z: 8, core: 2. Of those that a mesh axis runs over, the one named last changes fastest.
Arguments:
- tokens: bfloat16 [4096, 5120], P('expert', 'dp'), may hold values from -6 to 6
- out_grad: bfloat16 [4096, 5120], P('expert', 'dp'), may hold values from -0.59765625 to 0.59765625
- gate_values: float32 [4096, 8], P('expert'), may hold values from 0.05 to 0.5
- route_lists: int32 [4096, 8], P('expert'), may hold values from 0 to 15, all different within a row; in each aligned block of 128 rows (0 to 127, 128 to 255, ...) at most 72 rows name the same one
- expert_pairs: int32 [16], replicated, may hold values from 0 to 15, as said below
- gate_weight: bfloat16 [32, 5120, 1024], P('expert', 'dp'), as said below
- up_weight: bfloat16 [32, 5120, 1024], P('expert', 'dp'), as said below
- down_weight: bfloat16 [32, 1024, 5120], P('expert', None, 'dp'), as said below
Outputs:
- layer_output: bfloat16 [4096, 5120], P('expert', 'dp')
- token_grad: bfloat16 [4096, 5120], P('expert', 'dp')
- gate_value_grad: float32 [4096, 8], P('expert')
- gate_weight_grad: bfloat16 [32, 5120, 1024], P('expert', 'dp')
- up_weight_grad: bfloat16 [32, 5120, 1024], P('expert', 'dp')
- down_weight_grad: bfloat16 [32, 1024, 5120], P('expert', None, 'dp')
Inputs may be any that keep to these rules, and one draw needn't show every extreme that they name: `route_lists`: each token names 8 different experts; within each aligned block of 128 tokens no expert is named by more than 72 tokens. `expert_pairs`: a permutation; pair p is made of slots p and p + 16. `gate_weight`: slots p and p + 16 hold equal matrices, those of expert expert_pairs[p]. `up_weight`: slots p and p + 16 hold equal matrices. `down_weight`: slots p and p + 16 hold equal matrices.
All inputs are finite; a program needn't handle non-finite values.
Results may differ from a plain program's by a relative error of at most 0.023.
Values may be sent and summed in bfloat16 or wider, within the bound.
A program may use at most 128 MiB of HBM per device.

v0:
```python
import jax
import jax.numpy as jnp
from jax import lax
from jax.sharding import PartitionSpec as P

HALF = 36


def partner(x, axis, distance):
    return lax.ppermute(x, axis, [(i, i ^ 1 << distance) for i in range(lax.axis_size(axis))])


def shards(
    tokens, out_grad, gate_values, route_lists, expert_pairs, gate_weight, up_weight, down_weight
):
    tok_rows, width_dev = tokens.shape
    top_count = route_lists.shape[1]
    slot_count = lax.axis_size("expert")
    pair_count = slot_count // 2
    swap_bit = slot_count.bit_length() - 2
    contract_first = (((0,), (0,)), ((), ()))
    contract_second = (((1,), (1,)), ((), ()))
    catalog = jnp.arange(pair_count, dtype=jnp.int32)
    chosen = (route_lists[:, :, None] == catalog[None, None, :]).astype(jnp.int32)
    present = jnp.sum(chosen, axis=1)
    before = jnp.cumsum(present, axis=0) - present
    position = jnp.sum(chosen * before[:, None, :], axis=2)
    owner_pair = jnp.sum(
        jnp.where(
            route_lists[:, :, None] == expert_pairs[None, None, :], catalog[None, None, :], 0
        ),
        axis=2,
    )
    is_upper = (position >= HALF).astype(jnp.int32)
    target = (owner_pair + pair_count * is_upper) * HALF + position - HALF * is_upper
    capacity = slot_count * HALF
    flat_count = tok_rows * top_count
    slot_table = (
        jnp.full((capacity,), flat_count, jnp.int32)
        .at[target.reshape(-1)]
        .set(jnp.arange(flat_count, dtype=jnp.int32))
    )
    token_of = jnp.where(slot_table < flat_count, slot_table // top_count, tok_rows)
    padded_tokens = jnp.concatenate([tokens, jnp.zeros((1, width_dev), jnp.bfloat16)], axis=0)
    scaled_cot = (
        (gate_values[:, :, None] * out_grad.astype(jnp.float32)[:, None, :])
        .astype(jnp.bfloat16)
        .reshape(flat_count, width_dev)
    )
    padded_cot = jnp.concatenate([scaled_cot, jnp.zeros((1, width_dev), jnp.bfloat16)], axis=0)
    sent_tokens = padded_tokens[token_of].reshape(slot_count, HALF, width_dev)
    sent_cot = padded_cot[slot_table].reshape(slot_count, HALF, width_dev)
    got_tokens, got_cot = (
        lax.all_to_all(sent_tokens, "expert", split_axis=0, concat_axis=0, tiled=True),
        lax.all_to_all(sent_cot, "expert", split_axis=0, concat_axis=0, tiled=True),
    )
    row_total = slot_count * HALF
    rows_in = got_tokens.reshape(row_total, width_dev)
    cot_rows = got_cot.reshape(row_total, width_dev)
    w_gate = gate_weight[0]
    w_up = up_weight[0]
    w_down = down_weight[0]
    part_gate = jnp.dot(rows_in, w_gate, preferred_element_type=jnp.float32)
    part_up = jnp.dot(rows_in, w_up, preferred_element_type=jnp.float32)
    gate_pre, up_pre = (
        lax.psum(part_gate.astype(jnp.bfloat16), "dp").astype(jnp.float32),
        lax.psum(part_up.astype(jnp.bfloat16), "dp").astype(jnp.float32),
    )
    hidden = (jax.nn.silu(gate_pre) * up_pre).astype(jnp.bfloat16)
    expert_out = jnp.dot(hidden, w_down, preferred_element_type=jnp.float32).astype(jnp.bfloat16)
    grad_down = lax.dot_general(
        hidden, cot_rows, contract_first, preferred_element_type=jnp.float32
    ).astype(jnp.bfloat16)
    back_part = lax.dot_general(
        cot_rows, w_down, contract_second, preferred_element_type=jnp.float32
    )
    hidden_grad = lax.psum(back_part.astype(jnp.bfloat16), "dp").astype(jnp.float32)
    sigmoid_gate = jax.nn.sigmoid(gate_pre)
    up_grad = (hidden_grad * gate_pre * sigmoid_gate).astype(jnp.bfloat16)
    pre_grad = (
        hidden_grad * up_pre * sigmoid_gate * (1.0 + gate_pre * (1.0 - sigmoid_gate))
    ).astype(jnp.bfloat16)
    row_input_grad = (
        lax.dot_general(pre_grad, w_gate, contract_second, preferred_element_type=jnp.float32)
        + lax.dot_general(up_grad, w_up, contract_second, preferred_element_type=jnp.float32)
    ).astype(jnp.bfloat16)
    grad_gate = lax.dot_general(
        rows_in, pre_grad, contract_first, preferred_element_type=jnp.float32
    ).astype(jnp.bfloat16)
    grad_up = lax.dot_general(
        rows_in, up_grad, contract_first, preferred_element_type=jnp.float32
    ).astype(jnp.bfloat16)
    partner_gate, partner_up, partner_down = partner(
        (grad_gate, grad_up, grad_down), "expert", swap_bit
    )
    back_out, back_grad = (
        lax.all_to_all(
            expert_out.reshape(slot_count, HALF, width_dev),
            "expert",
            split_axis=0,
            concat_axis=0,
            tiled=True,
        ),
        lax.all_to_all(
            row_input_grad.reshape(slot_count, HALF, width_dev),
            "expert",
            split_axis=0,
            concat_axis=0,
            tiled=True,
        ),
    )
    out_each = back_out.reshape(capacity, width_dev)[target].astype(jnp.float32)
    grad_each = back_grad.reshape(capacity, width_dev)[target].astype(jnp.float32)
    layer_output = jnp.sum(gate_values[:, :, None] * out_each, axis=1).astype(jnp.bfloat16)
    token_grad = jnp.sum(grad_each, axis=1).astype(jnp.bfloat16)
    inner_dots = jnp.sum(out_grad.astype(jnp.float32)[:, None, :] * out_each, axis=2)
    gate_value_grad = lax.psum(inner_dots, "dp")
    gate_weight_grad = (grad_gate.astype(jnp.float32) + partner_gate.astype(jnp.float32)).astype(
        jnp.bfloat16
    )[None]
    up_weight_grad = (grad_up.astype(jnp.float32) + partner_up.astype(jnp.float32)).astype(
        jnp.bfloat16
    )[None]
    down_weight_grad = (grad_down.astype(jnp.float32) + partner_down.astype(jnp.float32)).astype(
        jnp.bfloat16
    )[None]
    return (
        layer_output,
        token_grad,
        gate_value_grad,
        gate_weight_grad,
        up_weight_grad,
        down_weight_grad,
    )


def solution(mesh):
    placed = (
        P("expert", "dp"),
        P("expert", "dp"),
        P("expert", None),
        P("expert", None),
        P(),
        P("expert", "dp", None),
        P("expert", "dp", None),
        P("expert", None, "dp"),
    )
    return jax.shard_map(
        shards,
        mesh=mesh,
        in_specs=placed,
        out_specs=(
            P("expert", "dp"),
            P("expert", "dp"),
            P("expert", None),
            P("expert", "dp", None),
            P("expert", "dp", None),
            P("expert", None, "dp"),
        ),
        check_vma=False,
    )
```

profile of v0, /device:TPU:8, one launch (start us, length us, event | category | flops | bytes accessed | tf_op | source)
XLA Modules:
  0.0 448.8 jit_solution(12803808135160498358)
XLA Ops:
  7.2 0.9 select_reduce_fusion.1
  8.4 0.7 select_reduce_fusion
  9.6 4.3 scatter_custom_fusion
  13.9 0.9 concatenate.6
  14.9 4.5 %gather_fusion = bf16[1152,640]{1,0:T(8,128)(2,1)S(1)} fusion(bf16[129,640]{1,0:T(8,128)(2,1)S(1)} %concatenate.6, s32[2048]{0:T(1024)S(1)} %get-tuple-element.30), kind=kCustom, calls=%fused_computation | custom fusion | bytes 2953728 | tf_op jit(solution)/shard_map/gather | solution.py:51
  19.4 1.3 reshape.143
  20.7 11.9 %all-to-all-start = ((bf16[32,36,640]{2,1,0:T(8,128)(2,1)}), bf16[32,36,640]{2,1,0:T(8,128)(2,1)}, u32[]{:S(2)}, u32[]{:S(2)}) async-start(bf16[32,36,640]{2,1,0:T(8,128)(2,1)} %reshape.143), calls=%async_computation | async-start | bytes 3276800 | tf_op jit(solution)/shard_map/all_to_all | solution.py:54
  33.2 4.8 %gather_fusion.2 = bf16[1152,640]{1,0:T(8,128)(2,1)} fusion(bf16[1025,640]{1,0:T(8,128)(2,1)S(1)} %concatenate.7, s32[2048]{0:T(1024)S(1)} %get-tuple-element.29), kind=kCustom, calls=%fused_computation.2 | custom fusion | bytes 2953728 | tf_op jit(solution)/shard_map/gather | solution.py:52
  38.0 3.3 reshape.147
  41.3 29.5 %all-to-all-done = bf16[32,36,640]{2,1,0:T(8,128)(2,1)} async-done(((bf16[32,36,640]{2,1,0:T(8,128)(2,1)}), bf16[32,36,640]{2,1,0:T(8,128)(2,1)}, u32[]{:S(2)}, u32[]{:S(2)}) %all-to-all-start) | async-done | bytes 1474592 | tf_op jit(solution)/shard_map/all_to_all | solution.py:54
  70.8 8.2 %all-to-all-start.2 = ((bf16[32,36,640]{2,1,0:T(8,128)(2,1)}), bf16[32,36,640]{2,1,0:T(8,128)(2,1)S(1)}, u32[]{:S(2)}, u32[]{:S(2)}) async-start(bf16[32,36,640]{2,1,0:T(8,128)(2,1)} %reshape.147), calls=%async_computation.2 | async-start | bytes 3276800 | tf_op jit(solution)/shard_map/all_to_all | solution.py:55
  79.2 3.3 reshape.144
  82.6 5.3 %convolution_convert_fusion.1 = bf16[1152,1024]{1,0:T(8,128)(2,1)} fusion(bf16[1152,640]{1,0:T(8,128)(2,1)} %reshape.144, bf16[1,640,1024]{2,1,0:T(8,128)(2,1)} %param.14), kind=kOutput, calls=%fused_computation.22 | convolution fusion | flops 1511129088 | bytes 5144576 | tf_op jit(solution)/shard_map/dot_general | solution.py:64
  87.9 3.5 convolution_convert_fusion.2
  91.4 25.3 %all-to-all-done.2 = bf16[32,36,640]{2,1,0:T(8,128)(2,1)S(1)} async-done(((bf16[32,36,640]{2,1,0:T(8,128)(2,1)}), bf16[32,36,640]{2,1,0:T(8,128)(2,1)S(1)}, u32[]{:S(2)}, u32[]{:S(2)}) %all-to-all-start.2) | async-done | bytes 1474592 | tf_op jit(solution)/shard_map/all_to_all | solution.py:55
  116.7 1.2 reshape.148
  117.9 5.3 %convolution_convert_fusion = bf16[1152,1024]{1,0:T(8,128)(2,1)} fusion(bf16[1152,640]{1,0:T(8,128)(2,1)} %reshape.148, bf16[1,1024,640]{2,1,0:T(8,128)(2,1)} %param.15), kind=kOutput, calls=%fused_computation.21 | convolution fusion | flops 1511129088 | bytes 5144576 | tf_op jit(solution)/shard_map/dot_general | solution.py:74
  123.3 96.2 %all-reduce.5.cloned.1.call-done = (bf16[1152,1024]{1,0:T(8,128)(2,1)}, bf16[1152,1024]{1,0:T(8,128)(2,1)}, bf16[1152,1024]{1,0:T(8,128)(2,1)}) async-done(((bf16[1152,1024]{1,0:T(8,128)(2,1)}, bf16[1152,1024]{1,0:T(8,128)(2,1)}, bf16[1152,1024]{1,0:T(8,128)(2,1)}), (bf16[1152,1024]{1,0:T(8,128)(2,1)}, bf16[1152,1024]{1,0:T(8,128)(2,1)}, bf16[1152,1024]{1,0:T(8,128)(2,1)})) %all-reduce.5.cloned.1.call-update) | async-done | bytes 7077904 | tf_op jit(solution)/shard_map/psum | solution.py:67
  219.4 5.7 %fusion.3 = (bf16[1152,1024]{1,0:T(8,128)(2,1)S(1)}, bf16[1152,1024]{1,0:T(8,128)(2,1)}) fusion(bf16[1152,1024]{1,0:T(8,128)(2,1)} %get-tuple-element.22, bf16[1152,1024]{1,0:T(8,128)(2,1)} %get-tuple-element.24, bf16[1152,1024]{1,0:T(8,128)(2,1)} %get-tuple-element.23), kind=kLoop, calls=%fused_computation.14 | loop fusion | flops 18874368 | bytes 11796480 | tf_op jit(solution)/shard_map/convert_element_type | solution.py:82
  225.1 1.5 copy-done.5
  226.6 2.0 fusion.21
  228.9 0.4 copy-done.12
  229.3 2.3 fusion.10
  231.6 1.4 reshape.149
  232.9 10.2 %all-to-all-start.3 = ((bf16[32,36,640]{2,1,0:T(8,128)(2,1)}), bf16[32,36,640]{2,1,0:T(8,128)(2,1)S(1)}, u32[]{:S(2)}, u32[]{:S(2)}) async-start(bf16[32,36,640]{2,1,0:T(8,128)(2,1)} %reshape.149), calls=%async_computation.3 | async-start | bytes 3276800 | tf_op jit(solution)/shard_map/all_to_all | solution.py:104
  243.1 4.0 convolution_convert_fusion.3
  247.1 1.3 reshape.145
  248.5 32.7 %all-to-all-done.3 = bf16[32,36,640]{2,1,0:T(8,128)(2,1)S(1)} async-done(((bf16[32,36,640]{2,1,0:T(8,128)(2,1)}), bf16[32,36,640]{2,1,0:T(8,128)(2,1)S(1)}, u32[]{:S(2)}, u32[]{:S(2)}) %all-to-all-start.3) | async-done | bytes 1474592 | tf_op jit(solution)/shard_map/all_to_all | solution.py:104
  281.2 8.0 %all-to-all-start.1 = ((bf16[32,36,640]{2,1,0:T(8,128)(2,1)}), bf16[32,36,640]{2,1,0:T(8,128)(2,1)}, u32[]{:S(2)}, u32[]{:S(2)}) async-start(bf16[32,36,640]{2,1,0:T(8,128)(2,1)} %reshape.145), calls=%async_computation.1 | async-start | bytes 3276800 | tf_op jit(solution)/shard_map/all_to_all | solution.py:97
  289.2 5.6 %convolution_convert_fusion.5 = bf16[640,1024]{1,0:T(8,128)(2,1)} fusion(bf16[1152,640]{1,0:T(8,128)(2,1)S(1)} %copy-done.8, bf16[1152,1024]{1,0:T(8,128)(2,1)} %get-tuple-element.23, bf16[1152,1024]{1,0:T(8,128)(2,1)} %get-tuple-element.24), kind=kOutput, calls=%fused_computation.37 | convolution fusion | flops 1520041984 | bytes 7503872 | tf_op jit(solution)/shard_map/dot_general | solution.py:90
  294.8 2.1 collective-permute-start.1
  296.9 3.0 convolution_convert_fusion.6
  299.9 1.4 collective-permute-start
  301.3 2.2 convolution_convert_fusion.4
  303.5 2.5 collective-permute-start.2
  306.2 34.9 %collective-permute-done.1 = bf16[640,1024]{1,0:T(8,128)(2,1)} collective-permute-done((bf16[640,1024]{1,0:T(8,128)(2,1)}, bf16[640,1024]{1,0:T(8,128)(2,1)}, u32[]{:S(2)}, u32[]{:S(2)}) %collective-permute-start.1) | collective-permute-done | bytes 1310752 | tf_op jit(solution)/shard_map/ppermute | solution.py:10
  341.1 3.3 fusion.15
  344.4 24.8 %collective-permute-done = bf16[640,1024]{1,0:T(8,128)(2,1)} collective-permute-done((bf16[640,1024]{1,0:T(8,128)(2,1)}, bf16[640,1024]{1,0:T(8,128)(2,1)}, u32[]{:S(2)}, u32[]{:S(2)}) %collective-permute-start) | collective-permute-done | bytes 1310752 | tf_op jit(solution)/shard_map/ppermute | solution.py:10
  369.2 3.3 fusion.14
  372.5 23.8 %collective-permute-done.2 = bf16[1024,640]{1,0:T(8,128)(2,1)} collective-permute-done((bf16[1024,640]{1,0:T(8,128)(2,1)S(1)}, bf16[1024,640]{1,0:T(8,128)(2,1)}, u32[]{:S(2)}, u32[]{:S(2)}) %collective-permute-start.2) | collective-permute-done | bytes 1310752 | tf_op jit(solution)/shard_map/ppermute | solution.py:10
  396.3 2.7 fusion.16
  399.3 4.0 gather_fusion.3
  403.4 1.5 bitcast_reduce_fusion
  404.9 2.3 reshape.146
  407.2 5.1 %gather_fusion.1 = bf16[1024,640]{1,0:T(8,128)(2,1)} fusion(bf16[1152,640]{1,0:T(8,128)(2,1)S(1)} %reshape.146, s32[1024]{0:T(1024)S(1)} %broadcast_clamp_fusion), kind=kCustom, calls=%fused_computation.1 | custom fusion | bytes 2625536 | tf_op jit(solution)/shard_map/gather | solution.py:112
  412.4 3.3 fusion.12
  415.6 25.7 %psum.31 = f32[128,8]{1,0:T(8,128)S(1)} all-reduce(f32[128,8]{1,0:T(8,128)S(1)} %get-tuple-element.18), channel_id=1, replica_groups=mesh['dp'=8,'expert'=32] {'dp'}, use_global_device_ids=true, to_apply=%region_11.12 | all-reduce | flops 1024 | bytes 8192 | tf_op jit(solution)/shard_map/psum | solution.py:117
  441.3 0.7 copy.31
  (49 shorter events, 2.5 us)
Async XLA Ops:
  7.2 80.7 %copy-start = (bf16[1,640,1024]{2,1,0:T(8,128)(2,1)S(1)}, bf16[1,640,1024]{2,1,0:T(8,128)(2,1)}, u32[]{:S(2)}) copy-start(bf16[1,640,1024]{2,1,0:T(8,128)(2,1)} %param.13) | copy-start | bytes 3932164
  20.7 11.9 %copy-start.11 = (f32[128,8]{0,1:T(8,128)S(1)}, f32[128,8]{0,1:T(8,128)}, u32[]{:S(2)}) copy-start(f32[128,8]{0,1:T(8,128)} %param.10) | copy-start | bytes 12292
  20.7 12.1 %copy-start.10 = (bf16[128,640]{1,0:T(8,128)(2,1)S(1)}, bf16[128,640]{1,0:T(8,128)(2,1)}, u32[]{:S(2)}) copy-start(bf16[128,640]{1,0:T(8,128)(2,1)} %param.9) | copy-start | bytes 491524
  20.7 50.1 %all-to-all-start = ((bf16[32,36,640]{2,1,0:T(8,128)(2,1)}), bf16[32,36,640]{2,1,0:T(8,128)(2,1)}, u32[]{:S(2)}, u32[]{:S(2)}) async-start(bf16[32,36,640]{2,1,0:T(8,128)(2,1)} %reshape.143), calls=%async_computation | async-start | bytes 3276800 | tf_op jit(solution)/shard_map/all_to_all | solution.py:54
  70.8 45.9 %all-to-all-start.2 = ((bf16[32,36,640]{2,1,0:T(8,128)(2,1)}), bf16[32,36,640]{2,1,0:T(8,128)(2,1)S(1)}, u32[]{:S(2)}, u32[]{:S(2)}) async-start(bf16[32,36,640]{2,1,0:T(8,128)(2,1)} %reshape.147), calls=%async_computation.2 | async-start | bytes 3276800 | tf_op jit(solution)/shard_map/all_to_all | solution.py:55
  79.0 140.4 %all-reduce.5.cloned.1.call-start = ((), (), s32[]{:S(2)}) async-start(), calls=%async_computation.4 | async-start | bytes 14155776 | tf_op jit(solution)/shard_map/psum | solution.py:67
  82.6 5.3 %copy-start.7 = (bf16[1152,640]{1,0:T(8,128)(2,1)S(1)}, bf16[1152,640]{1,0:T(8,128)(2,1)}, u32[]{:S(2)}) copy-start(bf16[1152,640]{1,0:T(8,128)(2,1)} %reshape.144) | copy-start | bytes 4423684
  225.1 1.5 copy-start.5
  226.6 2.0 copy-start.2
  226.6 2.4 copy-start.3
  226.6 2.7 copy-start.12
  232.9 48.2 %all-to-all-start.3 = ((bf16[32,36,640]{2,1,0:T(8,128)(2,1)}), bf16[32,36,640]{2,1,0:T(8,128)(2,1)S(1)}, u32[]{:S(2)}, u32[]{:S(2)}) async-start(bf16[32,36,640]{2,1,0:T(8,128)(2,1)} %reshape.149), calls=%async_computation.3 | async-start | bytes 3276800 | tf_op jit(solution)/shard_map/all_to_all | solution.py:104
  248.5 40.7 %copy-start.8 = (bf16[1152,640]{1,0:T(8,128)(2,1)S(1)}, bf16[1152,640]{1,0:T(8,128)(2,1)}, u32[]{:S(2)}) copy-start(bf16[1152,640]{1,0:T(8,128)(2,1)} %reshape.144) | copy-start | bytes 4423684
  281.2 123.7 %all-to-all-start.1 = ((bf16[32,36,640]{2,1,0:T(8,128)(2,1)}), bf16[32,36,640]{2,1,0:T(8,128)(2,1)}, u32[]{:S(2)}, u32[]{:S(2)}) async-start(bf16[32,36,640]{2,1,0:T(8,128)(2,1)} %reshape.145), calls=%async_computation.1 | async-start | bytes 3276800 | tf_op jit(solution)/shard_map/all_to_all | solution.py:97
  289.2 7.7 %copy-start.6 = (bf16[1152,1024]{1,0:T(8,128)(2,1)S(1)}, bf16[1152,1024]{1,0:T(8,128)(2,1)}, u32[]{:S(2)}) copy-start(bf16[1152,1024]{1,0:T(8,128)(2,1)} %copy-done.5) | copy-start | bytes 7077892
  294.8 6.5 %copy-start.4 = (bf16[1152,1024]{1,0:T(8,128)(2,1)S(1)}, bf16[1152,1024]{1,0:T(8,128)(2,1)}, u32[]{:S(2)}) copy-start(bf16[1152,1024]{1,0:T(8,128)(2,1)} %get-tuple-element.26) | copy-start | bytes 7077892
  294.8 6.5 %copy-start.9 = (bf16[1152,640]{1,0:T(8,128)(2,1)S(1)}, bf16[1152,640]{1,0:T(8,128)(2,1)}, u32[]{:S(2)}) copy-start(bf16[1152,640]{1,0:T(8,128)(2,1)} %reshape.148) | copy-start | bytes 4423684
  294.8 46.3 %collective-permute-start.1 = (bf16[640,1024]{1,0:T(8,128)(2,1)}, bf16[640,1024]{1,0:T(8,128)(2,1)}, u32[]{:S(2)}, u32[]{:S(2)}) collective-permute-start(bf16[640,1024]{1,0:T(8,128)(2,1)} %convolution_convert_fusion.5), channel_id=1, source_target_pairs={{0,16},{1,17},{2,18},{3,19},{4,20},{5,21},{6,22},{7,23},{8,24},{9,... | collective-permute-start | bytes 3932168 | tf_op jit(solution)/shard_map/ppermute | solution.py:10
  299.9 69.3 %collective-permute-start = (bf16[640,1024]{1,0:T(8,128)(2,1)}, bf16[640,1024]{1,0:T(8,128)(2,1)}, u32[]{:S(2)}, u32[]{:S(2)}) collective-permute-start(bf16[640,1024]{1,0:T(8,128)(2,1)} %convolution_convert_fusion.6), channel_id=1, source_target_pairs={{0,16},{1,17},{2,18},{3,19},{4,20},{5,21},{6,22},{7,23},{8,24},{9,... | collective-permute-start | bytes 3932168 | tf_op jit(solution)/shard_map/ppermute | solution.py:10
  303.5 92.8 %collective-permute-start.2 = (bf16[1024,640]{1,0:T(8,128)(2,1)S(1)}, bf16[1024,640]{1,0:T(8,128)(2,1)}, u32[]{:S(2)}, u32[]{:S(2)}) collective-permute-start(bf16[1024,640]{1,0:T(8,128)(2,1)S(1)} %convolution_convert_fusion.4), channel_id=1, source_target_pairs={{0,16},{1,17},{2,18},{3,19},{4,20},{5,21},{6,22},{7,23},{8,24},{9,... | collective-permute-start | bytes 3932168 | tf_op jit(solution)/shard_map/ppermute | solution.py:10
  407.2 34.8 %copy-start.1 = (bf16[1,640,1024]{2,1,0:T(8,128)(2,1)S(1)}, bf16[1,640,1024]{2,1,0:T(8,128)(2,1)}, u32[]{:S(2)}) copy-start(bf16[1,640,1024]{2,1,0:T(8,128)(2,1)} %param.13) | copy-start | bytes 3932164
Sparse Core Ops, SparseCore 0:
  123.4 96.0 all-reduce.4
where the time goes:
time: 450 us; the launch traced here: 449 us
  waiting for transfers between devices  267 us (59%)
  starting transfers between devices  44.4 us (10%)
  local copies, waits for them, and re-layouts  42.1 us (9%)
  matrix products  33.2 us (7%)
  blocking collectives  25.7 us (6%)
  other arithmetic  21.9 us (5%)
  between operations  14.3 us (3%)
    psum x1, waiting for transfers between devices, shards(): lax.psum(part_up.astype(jnp.bfloat16), 'dp').astype(jnp.float32)  96.2 us
    ppermute x3, waiting for transfers between devices, partner(): lax.ppermute(x, axis, [(i, i ^ 1 << distance) for i in range(lax.axis_siz...  83.5 us
    all_to_all x1, waiting for transfers between devices, shards(): lax.all_to_all(row_input_grad.reshape(slot_count, HALF, width_dev), 'expe...  32.7 us
    all_to_all x1, waiting for transfers between devices, shards(): lax.all_to_all(sent_tokens, 'expert', split_axis=0, concat_axis=0, tiled=...  29.5 us
    psum x1, blocking collectives, shards(): gate_value_grad = lax.psum(inner_dots, 'dp')  25.7 us
    all_to_all x1, waiting for transfers between devices, shards(): lax.all_to_all(sent_cot, 'expert', split_axis=0, concat_axis=0, tiled=True)  25.3 us
    all_to_all x1, starting transfers between devices, shards(): lax.all_to_all(sent_tokens, 'expert', split_axis=0, concat_axis=0, tiled=...  11.9 us
    all_to_all x1, starting transfers between devices, shards(): lax.all_to_all(row_input_grad.reshape(slot_count, HALF, width_dev), 'expe...  10.2 us
  transfers between devices with their start and end apart: 8, of which 7 were waited for; matrix products, arithmetic and copies ran while one was open for 12% of the time, Pallas kernels for 0%

commit v1 on v0

v1 whole, which is shorter than its diff:
```python
import jax
import jax.numpy as jnp
from jax import lax
from jax.experimental import pallas as pl
from jax.experimental.pallas import tpu as pltpu
from jax.sharding import PartitionSpec as P

F32 = jnp.float32
BF16 = jnp.bfloat16
TOK = 128
WID = 640
FF = 1024
CAP = 72
PAIR = 2 * CAP
GROUPS = 8
ROWS = GROUPS * PAIR
PU = 2 * FF + 128
RW = WID + 128
FAR = 4096.0

UP_SLOT = (2, 4, 6, 1)
DOWN_SLOT = (3, 5, 7, 1)
UP_CHAIN = (1, 7, 5, 3, 0)
DOWN_CHAIN = (1, 6, 4, 2, 0)

S_Z = 0
S_Y = 24
S_CG, S_XG = 32, 36
S_CH, S_XH = 40, 44
S_AX, S_AC = 48, 52
S_BX, S_BC = 56, 60
S_RO, S_RR = 64, 68
S_GD, S_GG = 72, 76
S_ZO = 84
N_SEM = 100


def dot(a, b):
    return jnp.dot(a, b, preferred_element_type=F32)


def dot_nt(a, b):
    return lax.dot_general(a, b, (((1,), (1,)), ((), ())), preferred_element_type=F32)


def dot_tn(a, b):
    return lax.dot_general(a, b, (((0,), (0,)), ((), ())), preferred_element_type=F32)


def layer(
    tok, og, route, gates, pairs, wg_in, wu_in, wd_in,
    out_o, grad_o, sdot_o, gg_o, gu_o, gd_o,
    wgu, wd, tab, tokz, ogz, rows, cot, rows_t, ysend, csend,
    part, crecv, xrecv, hpart, hcrecv, hxrecv, gpre, hid, pu,
    outb, outret, rigb, rigret, gd, gdr, gg, ggr,
    zo_part, zr_part, zo_send, zr_send, zo_recv, zr_recv,
    wsem, ssem, rsem,
):
    dp = lax.axis_index("dp")
    ex = lax.axis_index("expert")
    x, core = dp // 2, dp % 2
    y, z = ex // 8, ex % 8
    own_pair = (y % 2) * 8 + z
    oth_pair = (1 - y % 2) * 8 + z
    shard = dp

    def at(dx=0, dy=0, dz=0, other=False):
        c = 1 - core if other else core
        return (
            ((x + dx) % 4) * 2 + c,
            ((y + dy) % 4) * 8 + (z + dz) % 8,
        )

    def copy(src, dst, sem, device):
        return pltpu.make_async_remote_copy(
            src_ref=src,
            dst_ref=dst,
            send_sem=ssem.at[sem],
            recv_sem=rsem.at[sem],
            device_id=device,
            device_id_type=pl.DeviceIdType.MESH,
        )

    def group(g):
        return pl.ds(pl.multiple_of(g * PAIR, 16), PAIR)

    weights = [
        pltpu.make_async_copy(wg_in, wgu.at[:, 0:FF], wsem.at[0]),
        pltpu.make_async_copy(wu_in, wgu.at[:, FF : 2 * FF], wsem.at[1]),
        pltpu.make_async_copy(wd_in, wd, wsem.at[2]),
    ]
    for w in weights:
        w.start()

    barrier = pltpu.get_barrier_semaphore()
    peers = [at(dz=1), at(dz=-1), at(dy=1), at(dy=-1), at(dy=2)]
    peers += [at(dx=1), at(dx=2), at(dx=3), at(other=True)]
    for peer in peers:
        pl.semaphore_signal(barrier, inc=1, device_id=peer, device_id_type=pl.DeviceIdType.MESH)

    present = jnp.zeros((16, TOK), F32)
    weight = jnp.zeros((16, TOK), F32)
    pair_of = pairs[...]
    for k in range(8):
        named = route[k : k + 1, :] == pair_of
        present = present + jnp.where(named, 1.0, 0.0)
        weight = weight + jnp.where(named, gates[k : k + 1, :], 0.0)
    earlier = lax.broadcasted_iota(jnp.int32, (TOK, TOK), 0) < lax.broadcasted_iota(
        jnp.int32, (TOK, TOK), 1
    )
    before = dot(present.astype(BF16), jnp.where(earlier, 1.0, 0.0).astype(BF16))
    tab[0, 0:16, :] = jnp.where(present > 0.0, before, FAR)
    tab[0, 16:32, :] = weight
    tokz[0:TOK, :] = tok[...]
    ogz[0:TOK, :] = og[...]
    pl.semaphore_wait(barrier, len(peers))

    def block(ref, slot):
        return ref.at[slot] if ref is tab else ref.at[pl.ds(slot * TOK, TOK)]

    arrays = (tab, tokz, ogz)
    lengths = ((4, 3), (4, 3), (3, 4))
    pending = []

    def z_send(a, down, step):
        slots = DOWN_SLOT if down else UP_SLOT
        ref = arrays[a]
        if step == 0:
            src = tok if a == 1 else og if a == 2 else tab.at[0]
        else:
            src = block(ref, slots[step - 1])
        c = copy(
            src, block(ref, slots[step]), S_Z + (a * 2 + down) * 4 + step, at(dz=-1 if down else 1)
        )
        c.start()
        pending.append(c)

    def z_take(a, step):
        for down in (0, 1):
            if step < lengths[a][down]:
                slots = DOWN_SLOT if down else UP_SLOT
                dst = block(arrays[a], slots[step])
                copy(dst, dst, S_Z + (a * 2 + down) * 4 + step, at()).wait_recv()
                if step + 1 < lengths[a][down]:
                    z_send(a, down, step + 1)

    for a in range(3):
        for down in (0, 1):
            z_send(a, down, 0)

    row_no = lax.broadcasted_iota(jnp.int32, (PAIR, 2 * TOK), 0).astype(F32)

    def selection(j, pair):
        place = jnp.concatenate(
            [tab[2 * j, pl.ds(pair, 1), :], tab[2 * j + 1, pl.ds(pair, 1), :] + float(CAP)], axis=1
        )
        return row_no == place

    def weights_of(j, pair):
        return jnp.concatenate(
            [tab[2 * j, pl.ds(pair + 16, 1), :], tab[2 * j + 1, pl.ds(pair + 16, 1), :]], axis=1
        )

    def one_hot(sel):
        return jnp.where(sel, 1.0, 0.0).astype(BF16)

    for step in range(4):
        j = (step + 1) % 4
        dst_group = (4, 6, 5, 7)[step]
        toward = at(dy=-1 if step % 2 else 1)
        z_take(0, step)
        z_take(1, step)
        pick_own = selection(j, own_pair)
        pick_oth = selection(j, oth_pair)
        two = tokz[2 * TOK * j : 2 * TOK * (j + 1), :]
        ysend[j] = dot(one_hot(pick_oth), two).astype(BF16)
        c = copy(ysend.at[j], rows.at[group(dst_group)], S_Y + step, toward)
        c.start()
        pending.append(c)
        rows[j * PAIR : (j + 1) * PAIR, :] = dot(one_hot(pick_own), two).astype(BF16)
        z_take(2, step)
        two = ogz[2 * TOK * j : 2 * TOK * (j + 1), :]
        scale = jnp.sum(jnp.where(pick_oth, weights_of(j, oth_pair), 0.0), axis=1, keepdims=True)
        csend[j] = (dot(one_hot(pick_oth), two) * scale).astype(BF16)
        c = copy(csend.at[j], cot.at[group(dst_group)], S_Y + 4 + step, toward)
        c.start()
        pending.append(c)
        scale = jnp.sum(jnp.where(pick_own, weights_of(j, own_pair), 0.0), axis=1, keepdims=True)
        cot[j * PAIR : (j + 1) * PAIR, :] = (dot(one_hot(pick_own), two) * scale).astype(BF16)

    def reduce_terms(tiles, term, mine, from_core, from_x, s_core, s_x):
        def step(i, _):
            @pl.when(i < 4)
            def _():
                chip = (x + 1 + i) % 4
                span = pl.ds(pl.multiple_of(chip * 2 * PAIR, 16), 2 * PAIR)

                def tile(n, _):
                    cols = pl.ds(pl.multiple_of(n * 512, 512), 512)
                    mine[span, cols] = term(span, cols).astype(BF16)
                    return 0

                lax.fori_loop(0, tiles, tile, 0)
                copy(
                    mine.at[group(chip * 2 + 1 - core)],
                    from_core.at[chip],
                    s_core + i,
                    at(other=True),
                ).start()

            @pl.when(i >= 1)
            def _():
                chip = (x + i) % 4
                copy(from_core.at[chip], from_core.at[chip], s_core + i - 1, at()).wait_recv()
                g = group(chip * 2 + core)
                mine[g, :] = (mine[g, :].astype(F32) + from_core[chip].astype(F32)).astype(BF16)

                @pl.when(i < 4)
                def _():
                    copy(
                        mine.at[g], from_x.at[i - 1], s_x + i - 1, (chip * 2 + core, ex)
                    ).start()

            return 0

        lax.fori_loop(0, 5, step, 0)

    for step in range(4):
        dst = rows.at[group((4, 6, 5, 7)[step])]
        copy(dst, dst, S_Y + step, at()).wait_recv()
    weights[0].wait()
    weights[1].wait()
    reduce_terms(
        4, lambda span, cols: dot(rows[span, :], wgu[:, cols]), part, crecv, xrecv, S_CG, S_XG
    )
    for step in range(4):
        dst = cot.at[group((4, 6, 5, 7)[step])]
        copy(dst, dst, S_Y + 4 + step, at()).wait_recv()
    weights[2].wait()
    reduce_terms(
        2, lambda span, cols: dot_nt(cot[span, :], wd[cols, :]), hpart, hcrecv, hxrecv, S_CH, S_XH
    )

    mine = group(shard)
    for i in range(3):
        copy(xrecv.at[i], xrecv.at[i], S_XG + i, at()).wait_recv()

    def total(src, recv, cols):
        v = src[mine, cols].astype(F32)
        for i in range(3):
            v = v + recv[i, :, cols].astype(F32)
        return v

    def forward(n, _):
        cols = pl.ds(pl.multiple_of(n * 256, 256), 256)
        more = pl.ds(pl.multiple_of(FF + n * 256, 256), 256)
        gate_pre = total(part, xrecv, cols)
        up_pre = total(part, xrecv, more)
        gpre[:, cols] = gate_pre
        gpre[:, more] = up_pre
        hid[mine, cols] = (gate_pre * jax.nn.sigmoid(gate_pre) * up_pre).astype(BF16)
        return 0

    lax.fori_loop(0, 4, forward, 0)

    def spread(ref, s_x, s_core):
        for i in range(3):
            copy(ref.at[mine], ref.at[mine], s_x + i, at(dx=1 + i)).start()
        copy(ref.at[mine], ref.at[mine], s_core + 3, at(other=True)).start()

    def relay(ref, s_x, s_core):
        for i in range(3):
            g = ref.at[group(((x - 1 - i) % 4) * 2 + core)]
            copy(g, g, s_x + i, at()).wait_recv()
            copy(g, g, s_core + i, at(other=True)).start()
        for i in range(4):
            g = ref.at[group(((x - 1 - i) % 4) * 2 + 1 - core)]
            copy(g, g, s_core + i, at()).wait_recv()

    def spread_done(ref, s_x, s_core):
        g = ref.at[mine]
        for i in range(3):
            copy(g, g, s_x + i, at()).wait_send()
        for i in range(4):
            copy(g, g, s_core + i, at()).wait_send()

    spread(hid, S_AX, S_AC)
    for i in range(3):
        copy(hxrecv.at[i], hxrecv.at[i], S_XH + i, at()).wait_recv()

    def backward(n, acc):
        cols = pl.ds(pl.multiple_of(n * 256, 256), 256)
        more = pl.ds(pl.multiple_of(FF + n * 256, 256), 256)
        gate_pre = gpre[:, cols]
        up_pre = gpre[:, more]
        back = total(hpart, hxrecv, cols)
        s = jax.nn.sigmoid(gate_pre)
        act = gate_pre * s
        pu[mine, more] = (back * act).astype(BF16)
        pu[mine, cols] = (back * up_pre * s * (1.0 + gate_pre * (1.0 - s))).astype(BF16)
        return acc + jnp.sum(back * act * up_pre, axis=1, keepdims=True)

    sdot = lax.fori_loop(0, 4, backward, jnp.zeros((PAIR, 1), F32))
    sdot_hi = sdot.astype(BF16).astype(F32)
    lane = lax.broadcasted_iota(jnp.int32, (PAIR, 128), 1)
    slab = jnp.where(lane == own_pair, sdot_hi, 0.0) + jnp.where(
        lane == own_pair + 16, sdot - sdot_hi, 0.0
    )
    pu[mine, 2 * FF : PU] = slab.astype(BF16)
    spread(pu, S_BX, S_BC)
    rows_t[...] = rows[...].T

    relay(hid, S_AX, S_AC)
    back_to = ((4, 1, -1), (5, 3, -1), (6, 2, 1), (7, 0, 1))

    def expert_out(m, _):
        span = pl.ds(pl.multiple_of(((m + 2) % 4) * 2 * PAIR, 16), 2 * PAIR)
        outb[span, :] = dot(hid[span, :], wd[...]).astype(BF16)
        return 0

    lax.fori_loop(0, 4, expert_out, 0)
    for n, (g, j, dy) in enumerate(back_to):
        c = copy(outb.at[group(g)], outret.at[j], S_RO + n, at(dy=dy))
        c.start()
        pending.append(c)

    def down_grad(n, _):
        cols = pl.ds(pl.multiple_of(n * 256, 256), 256)
        gd[n] = dot_tn(hid[:, cols], cot[...]).astype(BF16)
        copy(gd.at[n], gdr.at[n], S_GD + n, at(dy=2)).start()
        return 0

    lax.fori_loop(0, 4, down_grad, 0)

    relay(pu, S_BX, S_BC)

    def input_grad(m, _):
        span = pl.ds(pl.multiple_of(((m + 2) % 4) * 2 * PAIR, 16), 2 * PAIR)
        rigb[span, 0:WID] = dot_nt(pu[span, 0 : 2 * FF], wgu[...]).astype(BF16)
        rigb[span, WID:RW] = pu[span, 2 * FF : PU]
        return 0

    lax.fori_loop(0, 4, input_grad, 0)
    for n, (g, j, dy) in enumerate(back_to):
        c = copy(rigb.at[group(g)], rigret.at[j], S_RR + n, at(dy=dy))
        c.start()
        pending.append(c)

    def in_grad(n, _):
        cols = pl.ds(pl.multiple_of(n * 256, 256), 256)
        gg[n] = dot(rows_t[...], pu[:, cols]).astype(BF16)
        copy(gg.at[n], ggr.at[n], S_GG + n, at(dy=2)).start()
        return 0

    lax.fori_loop(0, 8, in_grad, 0)

    for n, (g, j, dy) in enumerate(back_to):
        copy(outret.at[j], outret.at[j], S_RO + n, at()).wait_recv()
        copy(rigret.at[j], rigret.at[j], S_RR + n, at()).wait_recv()
    for j in range(4):
        outs = jnp.zeros((2 * TOK, WID), F32)
        grads = jnp.zeros((2 * TOK, RW), F32)
        for pair, o, r in (
            (own_pair, outb[j * PAIR : (j + 1) * PAIR, :], rigb[j * PAIR : (j + 1) * PAIR, :]),
            (oth_pair, outret[j], rigret[j]),
        ):
            sel = selection(j, pair)
            w = jnp.where(sel, weights_of(j, pair), 0.0)
            hi = w.astype(BF16)
            lo = (w - hi.astype(F32)).astype(BF16)
            outs = outs + dot_tn(hi, o) + dot_tn(lo, o)
            grads = grads + dot_tn(one_hot(sel), r)
        zo_part[2 * j] = outs[0:TOK]
        zo_part[2 * j + 1] = outs[TOK:]
        zr_part[2 * j] = grads[0:TOK]
        zr_part[2 * j + 1] = grads[TOK:]

    chains = []
    for a, (own, send, recv) in enumerate(
        ((zo_part, zo_send, zo_recv), (zr_part, zr_send, zr_recv))
    ):
        for down in (0, 1):
            slots = DOWN_CHAIN if down else UP_CHAIN
            if down != a:
                slots = slots[1:]
            chains.append((own, send, recv, down, slots, S_ZO + (a * 2 + down) * 4))
    for step in range(5):
        for own, send, recv, down, slots, sem in chains:
            if step >= len(slots) - 1:
                continue
            v = own[slots[step]]
            if step:
                prev = recv.at[down * 4 + step - 1]
                copy(prev, prev, sem + step - 1, at()).wait_recv()
                v = v + prev[...].astype(F32)
            send[down * 4 + step] = v.astype(BF16)
            c = copy(
                send.at[down * 4 + step],
                recv.at[down * 4 + step],
                sem + step,
                at(dz=-1 if down else 1),
            )
            c.start()
            pending.append(c)
    finals = []
    for a in (0, 1):
        own = chains[2 * a][0]
        v = own[0]
        for own, send, recv, down, slots, sem in chains[2 * a : 2 * a + 2]:
            prev = recv.at[down * 4 + len(slots) - 2]
            copy(prev, prev, sem + len(slots) - 2, at()).wait_recv()
            v = v + prev[...].astype(F32)
        finals.append(v)
    out_o[...] = finals[0].astype(BF16)
    grad_o[...] = finals[1][:, 0:WID].astype(BF16)
    sdot_o[...] = finals[1][:, WID:RW]

    def add_down(n, _):
        copy(gdr.at[n], gdr.at[n], S_GD + n, at()).wait_recv()
        gd_o[pl.ds(pl.multiple_of(n * 256, 256), 256), :] = (
            gd[n].astype(F32) + gdr[n].astype(F32)
        ).astype(BF16)
        return 0

    lax.fori_loop(0, 4, add_down, 0)

    def add_in(out, base):
        def body(n, _):
            m = base + n
            copy(ggr.at[m], ggr.at[m], S_GG + m, at()).wait_recv()
            out[:, pl.ds(pl.multiple_of(n * 256, 256), 256)] = (
                gg[m].astype(F32) + ggr[m].astype(F32)
            ).astype(BF16)
            return 0

        lax.fori_loop(0, 4, body, 0)

    add_in(gg_o, 0)
    add_in(gu_o, 4)

    for c in pending:
        c.wait_send()
    for i in range(4):
        copy(crecv.at[i], crecv.at[i], S_CG + i, at()).wait_send()
        copy(hcrecv.at[i], hcrecv.at[i], S_CH + i, at()).wait_send()
        copy(gd.at[i], gd.at[i], S_GD + i, at()).wait_send()
    for i in range(3):
        copy(xrecv.at[i], xrecv.at[i], S_XG + i, at()).wait_send()
        copy(hxrecv.at[i], hxrecv.at[i], S_XH + i, at()).wait_send()
    for i in range(8):
        copy(gg.at[i], gg.at[i], S_GG + i, at()).wait_send()
    spread_done(hid, S_AX, S_AC)
    spread_done(pu, S_BX, S_BC)


def shards(tokens, out_grad, gate_values, route_lists, expert_pairs, gate_weight, up_weight, down_weight):
    vmem = pl.BlockSpec(memory_space=pltpu.VMEM)
    hbm = pl.BlockSpec(memory_space=pl.ANY)
    sds = jax.ShapeDtypeStruct
    out, grad, sdot, gg, gu, gd = pl.pallas_call(
        layer,
        name="routed_layer",
        out_shape=(
            sds((TOK, WID), BF16),
            sds((TOK, WID), BF16),
            sds((TOK, 128), F32),
            sds((WID, FF), BF16),
            sds((WID, FF), BF16),
            sds((FF, WID), BF16),
        ),
        in_specs=[vmem] * 5 + [hbm] * 3,
        out_specs=(vmem,) * 6,
        scratch_shapes=[
            pltpu.VMEM((WID, 2 * FF), BF16),
            pltpu.VMEM((FF, WID), BF16),
            pltpu.VMEM((8, 32, TOK), F32),
            pltpu.VMEM((8 * TOK, WID), BF16),
            pltpu.VMEM((8 * TOK, WID), BF16),
            pltpu.VMEM((ROWS, WID), BF16),
            pltpu.VMEM((ROWS, WID), BF16),
            pltpu.VMEM((WID, ROWS), BF16),
            pltpu.VMEM((4, PAIR, WID), BF16),
            pltpu.VMEM((4, PAIR, WID), BF16),
            pltpu.VMEM((ROWS, 2 * FF), BF16),
            pltpu.VMEM((4, PAIR, 2 * FF), BF16),
            pltpu.VMEM((3, PAIR, 2 * FF), BF16),
            pltpu.VMEM((ROWS, FF), BF16),
            pltpu.VMEM((4, PAIR, FF), BF16),
            pltpu.VMEM((3, PAIR, FF), BF16),
            pltpu.VMEM((PAIR, 2 * FF), F32),
            pltpu.VMEM((ROWS, FF), BF16),
            pltpu.VMEM((ROWS, PU), BF16),
            pltpu.VMEM((ROWS, WID), BF16),
            pltpu.VMEM((4, PAIR, WID), BF16),
            pltpu.VMEM((ROWS, RW), BF16),
            pltpu.VMEM((4, PAIR, RW), BF16),
            pltpu.VMEM((4, 256, WID), BF16),
            pltpu.VMEM((4, 256, WID), BF16),
            pltpu.VMEM((8, WID, 256), BF16),
            pltpu.VMEM((8, WID, 256), BF16),
            pltpu.VMEM((8, TOK, WID), F32),
            pltpu.VMEM((8, TOK, RW), F32),
            pltpu.VMEM((8, TOK, WID), BF16),
            pltpu.VMEM((8, TOK, RW), BF16),
            pltpu.VMEM((8, TOK, WID), BF16),
            pltpu.VMEM((8, TOK, RW), BF16),
            pltpu.SemaphoreType.DMA((3,)),
            pltpu.SemaphoreType.DMA((N_SEM,)),
            pltpu.SemaphoreType.DMA((N_SEM,)),
        ],
        compiler_params=pltpu.CompilerParams(
            collective_id=0, has_side_effects=True, vmem_limit_bytes=67043328
        ),
    )(
        tokens,
        out_grad,
        route_lists.T,
        gate_values.T,
        expert_pairs.reshape(16, 1),
        gate_weight[0],
        up_weight[0],
        down_weight[0],
    )
    dots = sdot[:, 0:16] + sdot[:, 16:32]
    named = route_lists[:, :, None] == expert_pairs[None, None, :]
    gate_value_grad = jnp.sum(jnp.where(named, dots[:, None, :], 0.0), axis=2) / gate_values
    return out, grad, gate_value_grad, gg[None], gu[None], gd[None]


def solution(mesh):
    placed = (
        P("expert", "dp"),
        P("expert", "dp"),
        P("expert", None),
        P("expert", None),
        P(),
        P("expert", "dp", None),
        P("expert", "dp", None),
        P("expert", None, "dp"),
    )
    return jax.shard_map(
        shards,
        mesh=mesh,
        in_specs=placed,
        out_specs=(
            P("expert", "dp"),
            P("expert", "dp"),
            P("expert", None),
            P("expert", "dp", None),
            P("expert", "dp", None),
            P("expert", None, "dp"),
        ),
        check_vma=False,
    )
```

time: 450 us -> 261 us (0.58)
  waiting for transfers between devices: 267 us -> 0 us
  Pallas kernels: 0 us -> 245 us
  starting transfers between devices: 44.4 us -> 0 us
  matrix products: 33.2 us -> 0 us
  local copies, waits for them, and re-layouts: 42.1 us -> 9.99 us
  blocking collectives: 25.7 us -> 0 us
  other arithmetic: 21.9 us -> 3.08 us
  between operations: 14.3 us -> 0.66 us
    pallas_call x0 -> x1, Pallas kernels: none -> 245 us  [shards(): pl.pallas_call(layer, name='routed_layer', out_shape=(sds((TOK, WID), BF1...]
    psum x1 -> x0, waiting for transfers between devices: 96.2 us -> none  [shards(): lax.psum(part_up.astype(jnp.bfloat16), 'dp').astype(jnp.float32)]
    all_to_all x4 -> x0, waiting for transfers between devices: 87.6 us -> none  [the longest x1 32.7 us: shards(): lax.all_to_all(row_input_grad.reshape(slot_count, HALF, width_dev), 'expe...]
    ppermute x3 -> x0, waiting for transfers between devices: 83.5 us -> none  [partner(): lax.ppermute(x, axis, [(i, i ^ 1 << distance) for i in range(lax.axis_siz...]
    all_to_all x4 -> x0, starting transfers between devices: 38.2 us -> none  [the longest x1 11.9 us: shards(): lax.all_to_all(sent_tokens, 'expert', split_axis=0, concat_axis=0, tiled=...]
    dot_general x9 -> x0, matrix products: 33.2 us -> none  [the longest x1 5.62 us: shards(): lax.dot_general(rows_in, up_grad, contract_first, preferred_element_type=...]
    psum x1 -> x0, blocking collectives: 25.7 us -> none  [shards(): gate_value_grad = lax.psum(inner_dots, 'dp')]
    gather x4 -> x0, local copies, waits for them, and re-layouts: 18.5 us -> none  [the longest x1 5.14 us: shards(): out_each = back_out.reshape(capacity, width_dev)[target].astype(jnp.float32)]
  transfers between devices with their start and end apart: 8 -> 0, of which waited for: 7 -> 0; matrix products, arithmetic and copies ran while one was open for 12% -> 0% of each run, Pallas kernels for 0% -> 0%
where the time goes in v1:
time: 261 us; the launch traced here: 259 us
  Pallas kernels  245 us (94%)
  local copies, waits for them, and re-layouts  9.99 us (4%)
  other arithmetic  3.08 us (1%)
    pallas_call x1, Pallas kernels, shards(): pl.pallas_call(layer, name='routed_layer', out_shape=(sds((TOK, WID), BF1...  245 us
    unnamed x9, local copies, waits for them, and re-layouts  8.61 us

profile of v1, /device:TPU:8, one launch (start us, length us, event | category | flops | bytes accessed | tf_op | source)
XLA Modules:
  0.0 258.6 jit_solution(16317628820586976196)
XLA Ops:
  0.6 1.3 copy.16.pairs
  2.0 244.8 %routed_layer.1 = (bf16[128,640]{1,0:T(8,128)(2,1)}, bf16[128,640]{1,0:T(8,128)(2,1)}, f32[128,128]{1,0:T(8,128)}, bf16[640,1024]{1,0:T(8,128)(2,1)}, bf16[640,1...) custom-call(bf16[128,640]{1,0:T(8,128)(2,1)} %tok.1, bf16[128,640]{1,0:T(8,128)(2,1)} %og.1, s32[8,128]{1,0:T(8,128)} %bitcast.16, ...), custom_call_target="tpu_custom_call" | custom-call | tf_op jit(solution)/shard_map/routed_layer/pallas_call | solution.py:460
  246.8 1.0 slice_add_fusion
  247.8 0.1 copy.17
  247.9 0.8 select_reduce_fusion
  248.7 1.3 div.3
  249.9 1.6 copy.23
  251.5 1.6 copy.24
  253.1 0.0 copy-start.1
  253.1 2.6 copy.25
  255.7 0.0 copy-done.1
  255.7 0.0 copy-start
  255.7 1.1 copy.26
  256.8 0.7 copy-done
  257.5 1.1 copy.27
Async XLA Ops:
  253.1 2.6 copy-start.1
  255.7 1.8 copy-start

commit v2 on v1

--- a/solution.py
+++ b/solution.py
@@ -32,7 +32,8 @@
 S_RO, S_RR = 64, 68
 S_GD, S_GG = 72, 76
 S_ZO = 84
-N_SEM = 100
+S_RD, S_RG = 100, 104
+N_SEM = 112
 
 
 def dot(a, b):
@@ -52,7 +53,7 @@
     out_o, grad_o, sdot_o, gg_o, gu_o, gd_o,
     wgu, wd, tab, tokz, ogz, rows, cot, rows_t, ysend, csend,
     part, crecv, xrecv, hpart, hcrecv, hxrecv, gpre, hid, pu,
-    outb, outret, rigb, rigret, gd, gdr, gg, ggr,
+    outb, outret, rigb, rigret, gd, gdr, gg, ggr, gd_via, gg_via,
     zo_part, zr_part, zo_send, zr_send, zo_recv, zr_recv,
     wsem, ssem, rsem,
 ):
@@ -93,7 +94,7 @@
         w.start()
 
     barrier = pltpu.get_barrier_semaphore()
-    peers = [at(dz=1), at(dz=-1), at(dy=1), at(dy=-1), at(dy=2)]
+    peers = [at(dz=1), at(dz=-1), at(dy=1), at(dy=-1)]
     peers += [at(dx=1), at(dx=2), at(dx=3), at(other=True)]
     for peer in peers:
         pl.semaphore_signal(barrier, inc=1, device_id=peer, device_id_type=pl.DeviceIdType.MESH)
@@ -310,6 +311,11 @@
     spread(pu, S_BX, S_BC)
     rows_t[...] = rows[...].T
 
+    def pass_on(via, end, s_via, s_end, tiles):
+        for n in tiles:
+            copy(via.at[n], via.at[n], s_via + n, at()).wait_recv()
+            copy(via.at[n], end.at[n], s_end + n, at(dy=1 - 2 * (n % 2))).start()
+
     relay(hid, S_AX, S_AC)
     back_to = ((4, 1, -1), (5, 3, -1), (6, 2, 1), (7, 0, 1))
 
@@ -327,12 +333,13 @@
     def down_grad(n, _):
         cols = pl.ds(pl.multiple_of(n * 256, 256), 256)
         gd[n] = dot_tn(hid[:, cols], cot[...]).astype(BF16)
-        copy(gd.at[n], gdr.at[n], S_GD + n, at(dy=2)).start()
+        copy(gd.at[n], gd_via.at[n], S_RD + n, at(dy=1 - 2 * (n % 2))).start()
         return 0
 
     lax.fori_loop(0, 4, down_grad, 0)
 
     relay(pu, S_BX, S_BC)
+    pass_on(gd_via, gdr, S_RD, S_GD, (0, 1))
 
     def input_grad(m, _):
         span = pl.ds(pl.multiple_of(((m + 2) % 4) * 2 * PAIR, 16), 2 * PAIR)
@@ -349,10 +356,11 @@
     def in_grad(n, _):
         cols = pl.ds(pl.multiple_of(n * 256, 256), 256)
         gg[n] = dot(rows_t[...], pu[:, cols]).astype(BF16)
-        copy(gg.at[n], ggr.at[n], S_GG + n, at(dy=2)).start()
+        copy(gg.at[n], gg_via.at[n], S_RG + n, at(dy=1 - 2 * (n % 2))).start()
         return 0
 
     lax.fori_loop(0, 8, in_grad, 0)
+    pass_on(gd_via, gdr, S_RD, S_GD, (2, 3))
 
     for n, (g, j, dy) in enumerate(back_to):
         copy(outret.at[j], outret.at[j], S_RO + n, at()).wait_recv()
@@ -402,6 +410,8 @@
             )
             c.start()
             pending.append(c)
+        if step < 4:
+            pass_on(gg_via, ggr, S_RG, S_GG, (2 * step, 2 * step + 1))
     finals = []
     for a in (0, 1):
         own = chains[2 * a][0]
@@ -415,11 +425,18 @@
     grad_o[...] = finals[1][:, 0:WID].astype(BF16)
     sdot_o[...] = finals[1][:, WID:RW]
 
+    def store_down(n):
+        span = pl.ds(pl.multiple_of(n * 256, 256), 256)
+        return pltpu.make_async_copy(gdr.at[n], gd_o.at[span, :], wsem.at[3 + n])
+
+    def store_in(out, m, n):
+        cols = pl.ds(pl.multiple_of(n * 256, 256), 256)
+        return pltpu.make_async_copy(ggr.at[m], out.at[:, cols], wsem.at[7 + m])
+
     def add_down(n, _):
         copy(gdr.at[n], gdr.at[n], S_GD + n, at()).wait_recv()
-        gd_o[pl.ds(pl.multiple_of(n * 256, 256), 256), :] = (
-            gd[n].astype(F32) + gdr[n].astype(F32)
-        ).astype(BF16)
+        gdr[n] = (gd[n].astype(F32) + gdr[n].astype(F32)).astype(BF16)
+        store_down(n).start()
         return 0
 
     lax.fori_loop(0, 4, add_down, 0)
@@ -428,27 +445,33 @@
         def body(n, _):
             m = base + n
             copy(ggr.at[m], ggr.at[m], S_GG + m, at()).wait_recv()
-            out[:, pl.ds(pl.multiple_of(n * 256, 256), 256)] = (
-                gg[m].astype(F32) + ggr[m].astype(F32)
-            ).astype(BF16)
+            ggr[m] = (gg[m].astype(F32) + ggr[m].astype(F32)).astype(BF16)
+            store_in(out, m, n).start()
             return 0
 
         lax.fori_loop(0, 4, body, 0)
 
     add_in(gg_o, 0)
     add_in(gu_o, 4)
+
+    for n in range(4):
+        store_down(n).wait()
+        store_in(gg_o, n, n).wait()
+        store_in(gu_o, 4 + n, n).wait()
 
     for c in pending:
         c.wait_send()
     for i in range(4):
         copy(crecv.at[i], crecv.at[i], S_CG + i, at()).wait_send()
         copy(hcrecv.at[i], hcrecv.at[i], S_CH + i, at()).wait_send()
-        copy(gd.at[i], gd.at[i], S_GD + i, at()).wait_send()
+        copy(gd.at[i], gd.at[i], S_RD + i, at()).wait_send()
+        copy(gd_via.at[i], gd_via.at[i], S_GD + i, at()).wait_send()
     for i in range(3):
         copy(xrecv.at[i], xrecv.at[i], S_XG + i, at()).wait_send()
         copy(hxrecv.at[i], hxrecv.at[i], S_XH + i, at()).wait_send()
     for i in range(8):
-        copy(gg.at[i], gg.at[i], S_GG + i, at()).wait_send()
+        copy(gg.at[i], gg.at[i], S_RG + i, at()).wait_send()
+        copy(gg_via.at[i], gg_via.at[i], S_GG + i, at()).wait_send()
     spread_done(hid, S_AX, S_AC)
     spread_done(pu, S_BX, S_BC)
 
@@ -469,7 +492,7 @@
             sds((FF, WID), BF16),
         ),
         in_specs=[vmem] * 5 + [hbm] * 3,
-        out_specs=(vmem,) * 6,
+        out_specs=(vmem,) * 3 + (hbm,) * 3,
         scratch_shapes=[
             pltpu.VMEM((WID, 2 * FF), BF16),
             pltpu.VMEM((FF, WID), BF16),
@@ -498,13 +521,15 @@
             pltpu.VMEM((4, 256, WID), BF16),
             pltpu.VMEM((8, WID, 256), BF16),
             pltpu.VMEM((8, WID, 256), BF16),
+            pltpu.VMEM((4, 256, WID), BF16),
+            pltpu.VMEM((8, WID, 256), BF16),
             pltpu.VMEM((8, TOK, WID), F32),
             pltpu.VMEM((8, TOK, RW), F32),
             pltpu.VMEM((8, TOK, WID), BF16),
             pltpu.VMEM((8, TOK, RW), BF16),
             pltpu.VMEM((8, TOK, WID), BF16),
             pltpu.VMEM((8, TOK, RW), BF16),
-            pltpu.SemaphoreType.DMA((3,)),
+            pltpu.SemaphoreType.DMA((15,)),
             pltpu.SemaphoreType.DMA((N_SEM,)),
             pltpu.SemaphoreType.DMA((N_SEM,)),
         ],

time: 261 us -> 233 us (0.89)
  Pallas kernels: 245 us -> 216 us
    pallas_call x1, Pallas kernels: 245 us -> 216 us  [shards(): pl.pallas_call(layer, name='routed_layer', out_shape=(sds((TOK, WID), BF1...]
where the time goes in v2:
time: 233 us; the launch traced here: 230 us
  Pallas kernels  216 us (93%)
  local copies, waits for them, and re-layouts  9.99 us (4%)
  other arithmetic  3.08 us (1%)
    pallas_call x1, Pallas kernels, shards(): pl.pallas_call(layer, name='routed_layer', out_shape=(sds((TOK, WID), BF1...  216 us
    unnamed x9, local copies, waits for them, and re-layouts  8.61 us

profile of v2, /device:TPU:8, one launch (start us, length us, event | category | flops | bytes accessed | tf_op | source)
XLA Modules:
  0.0 229.6 jit_solution(18056328875621867747)
XLA Ops:
  0.6 1.3 copy.16.pairs
  2.0 215.9 %routed_layer.1 = (bf16[128,640]{1,0:T(8,128)(2,1)}, bf16[128,640]{1,0:T(8,128)(2,1)}, f32[128,128]{1,0:T(8,128)}, bf16[640,1024]{1,0:T(8,128)(2,1)}, bf16[640,1...) custom-call(bf16[128,640]{1,0:T(8,128)(2,1)} %tok.1, bf16[128,640]{1,0:T(8,128)(2,1)} %og.1, s32[8,128]{1,0:T(8,128)} %bitcast.16, ...), custom_call_target="tpu_custom_call" | custom-call | tf_op jit(solution)/shard_map/routed_layer/pallas_call | solution.py:483
  217.8 1.0 slice_add_fusion
  218.8 0.1 copy.17
  218.9 0.8 select_reduce_fusion
  219.7 1.3 div.3
  221.0 1.6 copy.23
  222.6 1.6 copy.24
  224.2 0.0 copy-start.1
  224.2 2.6 %copy.25 = bf16[1,640,1024]{2,1,0:T(8,128)(2,1)} copy(bf16[1,640,1024]{2,1,0:T(8,128)(2,1)} %bitcast.14) | data formatting | bytes 2621440
  226.7 0.0 copy-done.1
  226.7 0.0 copy-start
  226.7 1.1 copy.26
  227.8 0.7 copy-done
  228.5 1.1 copy.27
Async XLA Ops:
  224.2 2.6 %copy-start.1 = (bf16[640,1024]{1,0:T(8,128)(2,1)S(1)}, bf16[640,1024]{1,0:T(8,128)(2,1)}, u32[]{:S(2)}) copy-start(bf16[640,1024]{1,0:T(8,128)(2,1)} %get-tuple-element.16) | copy-start | bytes 3932164
  226.7 1.8 copy-start
